TPU v7x, 32 devices: a whole 2x2x4 slice. The times are simulated.
32 devices in a mesh: dp: 8 (over y, x, core), fsdp: 4 (over z).
Axes of the slice: x: 2, y: 2, z: 4, core: 2. Of those that a mesh axis runs over, the one named last changes fastest.
Arguments:
- tokens: bfloat16 [4096, 4096], P('dp'), may hold values from -6 to 6
- counts: int32 [8], P('dp'), may hold values from 256 to 512, as said below
- patch_index: int32 [4096], P('dp'), may hold values from 0 to 255
- clip_limit: float32 [], replicated, may hold values from 1024 to 8192
- norm_gain: float32 [4, 4096], replicated, may hold values from 0.25 to 1.75
- params: float32 [4, 4096, 4096], P(None, 'dp', 'fsdp'), may hold values from -0.09375 to 0.09375
- moments: float32 [4, 4096, 4096], P(None, 'dp', 'fsdp'), may hold values from -0.3 to 0.3
- seconds: float32 [4, 4096, 4096], P(None, 'dp', 'fsdp'), may hold values from 0.05 to 1
- gradients: float32 [4, 4096, 4096], P(None, 'dp', 'fsdp'), may hold values from -48 to 48
Outputs:
- params_new: float32 [4, 4096, 4096], P(None, 'dp', 'fsdp')
- moments_new: float32 [4, 4096, 4096], P(None, 'dp', 'fsdp')
- seconds_new: float32 [4, 4096, 4096], P(None, 'dp', 'fsdp')
- mixed: bfloat16 [4096, 4096], P('dp', 'fsdp')
Inputs may be any that keep to these rules, and one draw needn't show every extreme that they name: `counts`: at most 512, reached on some index of dp in every draw.
All inputs are finite; a program needn't handle non-finite values.
Results may differ from a plain program's by a relative error of at most 0.0095.
Values may be sent and summed in bfloat16 or wider, within the bound.
A program may use at most 192 MiB of HBM per device.

v0:
```python
import jax
import jax.numpy as jnp
from jax import lax
from jax.sharding import PartitionSpec as P

D = 4096
LAYERS = 4
GRID = 16
STEP = 40


beta_one = 0.9
beta_two = 0.95
adam_eps = 1e-08
learning_rate = 0.0024
weight_decay = 0.05
norm_eps = 1e-06


def position_code(patch_index):
    quarter = D // 4
    freqs = 1.0 / 10000.0 ** (jnp.arange(quarter, dtype=jnp.float32) / quarter)
    across = (patch_index // GRID).astype(jnp.float32)[:, None] * freqs[None, :]
    downward = (patch_index % GRID).astype(jnp.float32)[:, None] * freqs[None, :]
    return jnp.concatenate(
        [jnp.sin(across), jnp.cos(across), jnp.sin(downward), jnp.cos(downward)], axis=1
    )


def layer_norm(stream, gain_row):
    centre = jnp.mean(stream, axis=1, keepdims=True)
    shifted = stream - centre
    spread = jnp.mean(shifted * shifted, axis=1, keepdims=True)
    return (shifted * lax.rsqrt(spread + norm_eps) * gain_row[None, :]).astype(jnp.bfloat16)


def adam_update(params, moments, seconds, gradients, factor):
    clipped = gradients * factor
    moments_new = beta_one * moments + (1.0 - beta_one) * clipped
    seconds_new = beta_two * seconds + (1.0 - beta_two) * clipped * clipped
    direction = (
        moments_new
        / (1.0 - beta_one**STEP)
        / (jnp.sqrt(seconds_new / (1.0 - beta_two**STEP)) + adam_eps)
    )
    params_new = params - learning_rate * (direction + weight_decay * params)
    return (params_new, moments_new, seconds_new)


def advance(stream, branch, current, col_first, col_count):
    if current + 1 < LAYERS:
        widened = lax.all_gather(branch, "fsdp", axis=1, tiled=True)
        return stream + widened.astype(jnp.float32)
    return lax.dynamic_slice_in_dim(stream, col_first, col_count, 1) + branch.astype(jnp.float32)


def per_device(
    tokens, counts, patch_index, clip_limit, norm_gain, params, moments, seconds, gradients
):
    squares = lax.psum(jnp.sum(gradients * gradients), ("dp", "fsdp"))
    factor = jnp.minimum(1.0, clip_limit / (jnp.sqrt(squares) + 1e-06))
    params_new, moments_new, seconds_new = adam_update(params, moments, seconds, gradients, factor)
    weights = params_new.astype(jnp.bfloat16)
    tok_rows = tokens.shape[0]
    col_count = weights.shape[2]
    col_first = lax.axis_index("fsdp") * col_count
    valid = lax.broadcasted_iota(jnp.int32, (tok_rows, 1), 0) < counts[0]
    stream = jnp.where(valid, tokens.astype(jnp.float32) + position_code(patch_index), 0.0)
    gathered = lax.all_gather(weights, "dp", axis=1, tiled=True)
    for current in range(LAYERS):
        normed = layer_norm(stream, norm_gain[current])
        branch = jnp.dot(normed, gathered[current], preferred_element_type=jnp.float32).astype(
            jnp.bfloat16
        )
        stream = advance(stream, branch, current, col_first, col_count)
    mixed = jnp.where(valid, stream, 0.0).astype(jnp.bfloat16)
    return (params_new, moments_new, seconds_new, mixed)


def solution(mesh):
    in_specs = (
        P("dp", None),
        P("dp"),
        P("dp"),
        P(),
        P(),
        P(None, "dp", "fsdp"),
        P(None, "dp", "fsdp"),
        P(None, "dp", "fsdp"),
        P(None, "dp", "fsdp"),
    )
    out_specs = (
        P(None, "dp", "fsdp"),
        P(None, "dp", "fsdp"),
        P(None, "dp", "fsdp"),
        P("dp", "fsdp"),
    )
    return jax.shard_map(
        per_device, mesh=mesh, in_specs=in_specs, out_specs=out_specs, check_vma=False
    )
```

profile of v0, /device:TPU:0, one launch (start us, length us, event | category | flops | bytes accessed | tf_op | source)
XLA Modules:
  0.0 556.9 jit_solution(18285389573598532073)
XLA Ops:
  7.2 0.0 all-gather.5.cloned.1.call-start
  7.2 6.1 %multiply_reduce_fusion.4 = f32[]{:T(128)} fusion(f32[4,512,1024]{2,1,0:T(8,128)} %param.17), kind=kLoop, calls=%fused_computation.25 | loop fusion | flops 4194303 | bytes 8388612 | tf_op jit(solution)/shard_map/reduce_sum | solution.py:60
  14.0 42.2 %psum.7 = f32[]{:T(128)} all-reduce(f32[]{:T(128)} %multiply_reduce_fusion.4), channel_id=1, replica_groups=mesh['dp'=8,'fsdp'=4] {'dp','fsdp'}, use_global_device_ids=true, to_apply=%region_1.0 | all-reduce | flops 1 | bytes 8 | tf_op jit(solution)/shard_map/psum | solution.py:60
  57.0 0.0 copy-start.5
  57.0 20.8 %fusion.30 = (bf16[4,512,1024]{2,1,0:T(8,128)(2,1)}, f32[4,512,1024]{2,1,0:T(8,128)}, f32[4,512,1024]{2,1,0:T(8,128)}, f32[4,512,1024]{2,1,0:T(8,128)}) fusion(f32[4,512,1024]{2,1,0:T(8,128)} %param.14, f32[4,512,1024]{2,1,0:T(8,128)} %param.17, f32[]{:T(128)S(6)} %min.3, f32[4,512,1024]{2,1,0:T(8,128)} %param.15, f32[4,512,1024]{2,1,0:T(8,128)} %param.16), kind=kLoop, calls=%fused_computation.71 | loop fusion | flops 35651584 | bytes 62914564 | tf_op jit(solution)/shard_map/convert_element_type | solution.py:63
  77.8 0.0 all-gather.5.cloned.1.call-update
  77.8 0.2 all-gather.7.cloned.1.call-start
  78.0 0.0 copy-start.3
  78.9 0.0 copy-done.5
  78.9 14.7 %multiply_sine_fusion.1 = (f32[512,1024]{1,0:T(8,128)S(1)}, f32[512,1024]{1,0:T(8,128)S(1)}, f32[512,1024]{1,0:T(8,128)S(1)}, f32[512,1024]{1,0:T(8,128)S(1)}) fusion(f32[1024]{0:T(1024)S(1)} %negate_power_fusion, f32[512]{0:T(512)S(1)} %get-tuple-element.24, f32[512]{0:T(512)S(1)} %get-tuple-element.25), kind=kLoop, calls=%fused_computation.41 | loop fusion | flops 1048576 | bytes 8396800 | tf_op jit(solution)/shard_map/sin | solution.py:26
  93.7 0.0 copy-done.3
  93.7 1.7 fusion.28
  95.4 0.0 copy-start
  95.4 0.0 copy-start.4
  95.4 3.2 copy-done
  98.6 1.0 multiply_reduce_fusion.3
  99.6 0.0 copy-done.4
  99.6 139.0 %all-gather.5.cloned.1.call-done = bf16[4,4096,1024]{2,1,0:T(8,128)(2,1)} async-done(((bf16[4,512,1024]{2,1,0:T(8,128)(2,1)}), bf16[4,4096,1024]{2,1,0:T(8,128)(2,1)}) %all-gather.5.cloned.1.call-update) | async-done | bytes 33554448 | tf_op jit(solution)/shard_map/all_gather | solution.py:69
  238.6 11.3 %fusion.18 = bf16[512,1024]{1,0:T(8,128)(2,1)} fusion(bf16[4,4096,1024]{2,1,0:T(8,128)(2,1)} %all-gather.5.cloned.1.call-done, f32[512,4096]{1,0:T(8,128)} %copy-done, f32[4096]{0:T(1024)S(1)} %bitcast.33, f32[512]{0:T(512)S(1)} %add_rsqrt_fusion.3, f32[512]{0:T(512)S(1)} %broadcast_multiply_fusion.3), kind=kOutput, calls=%fused_computation.43 | convolution fusion | flops 4303880192 | bytes 17846272 | tf_op jit(solution)/shard_map/dot_general | solution.py:72
  249.9 0.0 all-gather.7.cloned.1.call-update
  249.9 0.0 all-gather.9.cloned.1.call-start
  250.0 80.8 %all-gather.7.cloned.1.call-done = bf16[512,4096]{1,0:T(8,128)(2,1)} async-done(((bf16[512,1024]{1,0:T(8,128)(2,1)}), bf16[512,4096]{1,0:T(8,128)(2,1)}) %all-gather.7.cloned.1.call-update) | async-done | bytes 4194320 | tf_op jit(solution)/shard_map/all_gather | solution.py:52
  330.8 0.0 copy-start.2
  330.8 0.0 slice-start
  330.8 5.6 %fusion.22 = f32[512]{0:T(512)S(1)} fusion(f32[512,4096]{1,0:T(8,128)} %copy-done, bf16[512,4096]{1,0:T(8,128)(2,1)} %all-gather.7.cloned.1.call-done), kind=kLoop, calls=%fused_computation.47 | loop fusion | flops 6290944 | bytes 12584960 | tf_op jit(solution)/shard_map/reduce_sum | solution.py:31
  336.4 0.1 copy-done.2
  336.6 0.0 slice-start.1
  336.6 5.2 multiply_reduce_fusion.2
  341.8 0.0 slice-done
  341.8 0.0 slice-done.1
  341.8 9.2 %fusion.19 = bf16[512,1024]{1,0:T(8,128)(2,1)} fusion(bf16[4,4096,1024]{2,1,0:T(8,128)(2,1)} %all-gather.5.cloned.1.call-done, f32[4096]{0:T(1024)S(1)} %bitcast.32, f32[512]{0:T(512)S(1)} %add_rsqrt_fusion.2, f32[512]{0:T(512)S(1)} %broadcast_multiply_fusion.2, f32[512,4096]{1,0:T(8,128)S(1)} %bitcast.29, bf16[512,4096]{1,0:T(8,128)(2,1)S(1)} %copy-done.2), kind=kOutput, calls=%fused_computation.44 | convolution fusion | flops 4308074496 | bytes 22040576 | tf_op jit(solution)/shard_map/dot_general | solution.py:72
  351.0 0.0 all-gather.9.cloned.1.call-update
  351.1 0.3 all-gather.11.cloned.1.call-start
  351.4 79.1 %all-gather.9.cloned.1.call-done = bf16[512,4096]{1,0:T(8,128)(2,1)} async-done(((bf16[512,1024]{1,0:T(8,128)(2,1)}), bf16[512,4096]{1,0:T(8,128)(2,1)}) %all-gather.9.cloned.1.call-update) | async-done | bytes 4194320 | tf_op jit(solution)/shard_map/all_gather | solution.py:52
  430.4 10.3 %fusion.27 = (f32[512]{0:T(512)S(1)}, f32[512,4096]{1,0:T(8,128)}) fusion(bf16[512,4096]{1,0:T(8,128)(2,1)} %all-gather.9.cloned.1.call-done, f32[512,4096]{1,0:T(8,128)} %copy-done, bf16[512,4096]{1,0:T(8,128)(2,1)} %all-gather.7.cloned.1.call-done), kind=kLoop, calls=%fused_computation.69 | loop fusion | flops 10485248 | bytes 25167872 | tf_op jit(solution)/shard_map/reduce_sum | solution.py:31
  440.7 0.0 copy-start.1
  440.8 4.5 multiply_reduce_fusion.1
  445.3 1.3 copy-done.1
  446.5 9.0 %fusion.20 = bf16[512,1024]{1,0:T(8,128)(2,1)} fusion(bf16[4,4096,1024]{2,1,0:T(8,128)(2,1)} %all-gather.5.cloned.1.call-done, f32[512,4096]{1,0:T(8,128)S(1)} %copy-done.1, f32[4096]{0:T(1024)S(1)} %bitcast.31, f32[512]{0:T(512)S(1)} %add_rsqrt_fusion.1, f32[512]{0:T(512)S(1)} %broadcast_multiply_fusion.1), kind=kOutput, calls=%fused_computation.45 | convolution fusion | flops 4303880192 | bytes 17846272 | tf_op jit(solution)/shard_map/dot_general | solution.py:72
  455.6 0.0 all-gather.11.cloned.1.call-update
  455.6 79.4 %all-gather.11.cloned.1.call-done = bf16[512,4096]{1,0:T(8,128)(2,1)} async-done(((bf16[512,1024]{1,0:T(8,128)(2,1)}), bf16[512,4096]{1,0:T(8,128)(2,1)}) %all-gather.11.cloned.1.call-update) | async-done | bytes 4194320 | tf_op jit(solution)/shard_map/all_gather | solution.py:52
  535.0 5.5 fusion.26
  540.5 1.0 multiply_reduce_fusion
  541.4 8.9 %select_convert_fusion = bf16[512,1024]{1,0:T(8,128)(2,1)} fusion(f32[512,4096]{1,0:T(8,128)S(1)} %get-tuple-element.5, s32[]{:T(128)S(6)} %select_n.26, bf16[4,4096,1024]{2,1,0:T(8,128)(2,1)} %all-gather.5.cloned.1.call-done, f32[4096]{0:T(1024)S(1)} %bitcast.30, f32[512]{0:T(512)S(1)} %add_rsqrt_fusion, f32[512]{0:T(512)S(1)} %broadcast_multiply_fusion, ...), kind=kOutput, calls=%fused_computation.42 | convolution fusion | flops 4305977344 | bytes 19943940 | tf_op jit(solution)/shard_map/dot_general | solution.py:72
  (13 shorter events, 0.1 us)
Async XLA Ops:
  7.2 231.5 %all-gather.5.cloned.1.call-start = ((), (), s32[]{:S(2)}) async-start(), calls=%async_computation | async-start | bytes 37748736 | tf_op jit(solution)/shard_map/all_gather | solution.py:69
  57.0 21.9 %copy-start.5 = (s32[512]{0:T(512)S(1)}, s32[512]{0:T(512)}, u32[]{:S(2)}) copy-start(s32[512]{0:T(512)} %param.11) | copy-start | bytes 6148
  77.8 253.0 %all-gather.7.cloned.1.call-start = ((), (), s32[]{:S(2)}) async-start(), calls=%async_computation.1 | async-start | bytes 5242880 | tf_op jit(solution)/shard_map/all_gather | solution.py:52
  78.0 15.6 %copy-start.3 = (bf16[512,4096]{1,0:T(8,128)(2,1)S(1)}, bf16[512,4096]{1,0:T(8,128)(2,1)}, u32[]{:S(2)}) copy-start(bf16[512,4096]{1,0:T(8,128)(2,1)} %param.9) | copy-start | bytes 12582916
  95.4 3.2 copy-start
  95.4 4.2 copy-start.4
  249.9 180.5 %all-gather.9.cloned.1.call-start = ((), (), s32[]{:S(2)}) async-start(), calls=%async_computation.2 | async-start | bytes 5242880 | tf_op jit(solution)/shard_map/all_gather | solution.py:52
  330.8 5.8 %copy-start.2 = (bf16[512,4096]{1,0:T(8,128)(2,1)S(1)}, bf16[512,4096]{1,0:T(8,128)(2,1)}, u32[]{:S(2)}) copy-start(bf16[512,4096]{1,0:T(8,128)(2,1)} %all-gather.7.cloned.1.call-done) | copy-start | bytes 12582916
  330.8 11.0 %slice-start = ((s8[8388608]{0:T(1024)(128)(4,1)}), s8[4194304]{0:T(1024)(128)(4,1)S(1)}, s32[]{:S(2)}) async-start(s8[8388608]{0:T(1024)(128)(4,1)} %bitcast.28), calls=%async_computation.4 | async-start | bytes 8388608
  336.6 5.2 slice-start.1
  351.1 183.9 %all-gather.11.cloned.1.call-start = ((), (), s32[]{:S(2)}) async-start(), calls=%async_computation.3 | async-start | bytes 5242880 | tf_op jit(solution)/shard_map/all_gather | solution.py:52
  440.7 5.8 %copy-start.1 = (f32[512,4096]{1,0:T(8,128)S(1)}, f32[512,4096]{1,0:T(8,128)}, u32[]{:S(2)}) copy-start(f32[512,4096]{1,0:T(8,128)} %get-tuple-element.7) | copy-start | bytes 25165828
Sparse Core Ops, SparseCore 0:
  77.9 160.6 all-gather.4
  250.0 80.7 all-gather.6
  351.2 79.2 all-gather.8
  455.7 79.2 all-gather.10
where the time goes:
time: 557 us
  waiting for transfers between devices  378 us (68%)
  other arithmetic  76.5 us (14%)
  blocking collectives  42.2 us (8%)
  matrix products  38.4 us (7%)
  between operations  16.1 us (3%)
    all_gather x3, waiting for transfers between devices, advance(): widened = lax.all_gather(branch, 'fsdp', axis=1, tiled=True)  239 us
    all_gather x1, waiting for transfers between devices, per_device(): gathered = lax.all_gather(weights, 'dp', axis=1, tiled=True)  139 us
    psum x1, blocking collectives, per_device(): squares = lax.psum(jnp.sum(gradients * gradients), ('dp', 'fsdp'))  42.2 us
    dot_general x4, matrix products, per_device(): jnp.dot(normed, gathered[current], preferred_element_type=jnp.float32)  38.4 us
    reduce_sum x4, other arithmetic, layer_norm(): centre = jnp.mean(stream, axis=1, keepdims=True)  23.1 us
    convert_element_type x1, other arithmetic, per_device(): weights = params_new.astype(jnp.bfloat16)  20.8 us
    sin x1, other arithmetic, position_code(): jnp.sin(across)  14.7 us
    reduce_sum x4, other arithmetic, layer_norm(): spread = jnp.mean(shifted * shifted, axis=1, keepdims=True)  11.6 us
  transfers between devices with their start and end apart: 4, of which 4 were waited for; matrix products, arithmetic and copies ran while one was open for 3% of the time, Pallas kernels for 0%

commit v1 on v0

v1 whole, which is shorter than its diff:
```python
import functools
import jax
import jax.numpy as jnp
from jax import lax
from jax.experimental import pallas as pl
from jax.experimental.pallas import tpu as pltpu
from jax.sharding import PartitionSpec as P

GRID = 16
STEP = 40

beta_one = 0.9
beta_two = 0.95
adam_eps = 1e-08
learning_rate = 0.0024
weight_decay = 0.05
norm_eps = 1e-06

MESH = pl.DeviceIdType.MESH
ANY = pl.BlockSpec(memory_space=pl.ANY)
VMEM = pl.BlockSpec(memory_space=pltpu.VMEM)
SMEM = pl.BlockSpec(memory_space=pltpu.SMEM)


def position_code(patch_index, width):
    quarter = width // 4
    freqs = 1.0 / 10000.0 ** (jnp.arange(quarter, dtype=jnp.float32) / quarter)
    across = (patch_index // GRID).astype(jnp.float32)[:, None] * freqs[None, :]
    downward = (patch_index % GRID).astype(jnp.float32)[:, None] * freqs[None, :]
    return jnp.concatenate(
        [jnp.sin(across), jnp.cos(across), jnp.sin(downward), jnp.cos(downward)], axis=1
    )


def adam_update(params, moments, seconds, gradients, factor):
    clipped = gradients * factor
    moments_new = beta_one * moments + (1.0 - beta_one) * clipped
    seconds_new = beta_two * seconds + (1.0 - beta_two) * clipped * clipped
    direction = (
        moments_new
        / (1.0 - beta_one**STEP)
        / (jnp.sqrt(seconds_new / (1.0 - beta_two**STEP)) + adam_eps)
    )
    params_new = params - learning_rate * (direction + weight_decay * params)
    return (params_new, moments_new, seconds_new)


def total_kernel(sizes, x_ref, o_ref, *scratch):
    names = ("dp", "fsdp")
    mid, got, send, recv = scratch[0], scratch[1:3], scratch[3:5], scratch[5:7]
    place = [lax.axis_index(name) for name in names]
    barrier = pltpu.get_barrier_semaphore()
    for axis in range(2):
        for step in range(1, sizes[axis]):
            pl.semaphore_signal(
                barrier,
                inc=1,
                device_id={names[axis]: lax.rem(place[axis] + step, sizes[axis])},
                device_id_type=MESH,
            )
    pl.semaphore_wait(barrier, sizes[0] + sizes[1] - 2)
    for axis in range(2):
        source = x_ref if axis == 0 else mid
        copies = []
        for step in range(1, sizes[axis]):
            copy = pltpu.make_async_remote_copy(
                src_ref=source,
                dst_ref=got[axis].at[place[axis]],
                send_sem=send[axis].at[step - 1],
                recv_sem=recv[axis].at[step - 1],
                device_id={names[axis]: lax.rem(place[axis] + step, sizes[axis])},
                device_id_type=MESH,
            )
            copy.start()
            copies.append(copy)
        got[axis][place[axis]] = source[...]
        for copy in copies:
            copy.wait()
        total = got[axis][0]
        for slot in range(1, sizes[axis]):
            total = total + got[axis][slot]
        if axis == 0:
            mid[...] = total
        else:
            o_ref[...] = total


def total_over_mesh(value, sizes):
    shape = (8, 128)
    total = pl.pallas_call(
        functools.partial(total_kernel, sizes),
        out_shape=jax.ShapeDtypeStruct(shape, jnp.float32),
        in_specs=[VMEM],
        out_specs=VMEM,
        scratch_shapes=[
            pltpu.VMEM(shape, jnp.float32),
            pltpu.VMEM((sizes[0],) + shape, jnp.float32),
            pltpu.VMEM((sizes[1],) + shape, jnp.float32),
        ]
        + [pltpu.SemaphoreType.DMA((max(size - 1, 1),)) for size in sizes] * 2,
        compiler_params=pltpu.CompilerParams(collective_id=0, has_side_effects=True),
        name="total",
    )(jnp.full(shape, value))
    return total[0, 0]


def layer_kernel(first, last, n, chunks, names, *refs):
    r = dict(zip(names, refs))
    place = lax.axis_index("fsdp")
    rows, width = r["stream"].shape
    cols = r["weights"].shape[1]
    part = rows // chunks
    depth = r["w"].shape[0] // 4

    def rows_of(c):
        return pl.ds(pl.multiple_of(c * part, part), part)

    def cols_of(owner):
        return pl.ds(pl.multiple_of(owner * cols, cols), cols)

    def take_stream(c):
        return pltpu.make_async_copy(
            r["stream"].at[rows_of(c)], r["s"].at[rows_of(c)], r["s_sem"].at[c]
        )

    def take_branch(c):
        return pltpu.make_async_copy(
            r["branch"].at[rows_of(c)], r["b"].at[rows_of(c)], r["b_sem"].at[c]
        )

    def take_weights(k):
        piece = pl.ds(k * depth, depth)
        return pltpu.make_async_copy(r["weights"].at[piece], r["w"].at[piece], r["w_sem"].at[k])

    def put_stream(c):
        return pltpu.make_async_copy(
            r["s"].at[rows_of(c)], r["stream_out"].at[rows_of(c)], r["so_sem"].at[c]
        )

    def put_own(c):
        return pltpu.make_async_copy(
            r["own"].at[rows_of(c)],
            r["branch_out"].at[rows_of(c), cols_of(place)],
            r["own_sem"].at[c],
        )

    def pass_on(way, hop, c):
        if hop == 0:
            owner = place
            source = r["own"].at[rows_of(c)]
        else:
            owner = place - hop if way == 0 else place + hop
            source = r["branch_out"].at[rows_of(c), cols_of(owner)]
        peer = lax.rem(place + 1, n) if way == 0 else lax.rem(place + n - 1, n)
        return pltpu.make_async_remote_copy(
            src_ref=source,
            dst_ref=r["branch_out"].at[rows_of(c), cols_of(owner)],
            send_sem=r["send"].at[way, hop, c],
            recv_sem=r["recv"].at[way, hop, c],
            device_id={"fsdp": peer},
            device_id_type=MESH,
        )

    def has_sent(way, hop):
        if way == 0:
            return jnp.logical_and(place < n - 1, place >= hop)
        return jnp.logical_and(place > 0, place + hop < n)

    def has_got(way, hop):
        return place >= hop + 1 if way == 0 else place + hop + 1 < n

    for c in range(chunks):
        take_stream(c).start()
        if not first:
            take_branch(c).start()
        if c == 0:
            for k in range(4):
                take_weights(k).start()

    if not last:
        barrier = pltpu.get_barrier_semaphore()
        for step in (1, n - 1):
            pl.semaphore_signal(
                barrier, inc=1, device_id={"fsdp": lax.rem(place + step, n)}, device_id_type=MESH
            )
        pl.semaphore_wait(barrier, 2)

    sub = 32
    tile = 256

    def chunk_body(c, carry):
        take_stream(c).wait()
        if not first:
            take_branch(c).wait()

        def norm_body(k, carry):
            at = pl.ds(pl.multiple_of(c * part + k * sub, sub), sub)
            x = r["s"][at]
            if not first:
                x = x + r["b"][at].astype(jnp.float32)
                r["s"][at] = x
            centre = jnp.sum(x, axis=1, keepdims=True) * (1.0 / width)
            shifted = x - centre
            spread = jnp.sum(shifted * shifted, axis=1, keepdims=True) * (1.0 / width)
            normed = shifted * lax.rsqrt(spread + norm_eps) * r["gain"][...]
            r["x"][pl.ds(pl.multiple_of(k * sub, sub), sub)] = normed.astype(jnp.bfloat16)
            return carry

        lax.fori_loop(0, part // sub, norm_body, 0)
        if "stream_out" in r:
            put_stream(c).start()

        @pl.when(c == 0)
        def _():
            for k in range(4):
                take_weights(k).wait()

        def dot_body(t, carry):
            at = pl.ds(pl.multiple_of(t * tile, tile), tile)
            out = jnp.dot(
                r["x"][...], r["w"][:, at], preferred_element_type=jnp.float32
            ).astype(jnp.bfloat16)
            if last:
                mine = pl.ds(pl.multiple_of(place * cols + t * tile, tile), tile)
                slot = c * part + lax.broadcasted_iota(jnp.int32, (part, tile), 0)
                total = r["s"][rows_of(c), mine] + out.astype(jnp.float32)
                total = jnp.where(slot < r["counts"][0], total, 0.0)
                r["mixed"][rows_of(c), at] = total.astype(jnp.bfloat16)
            else:
                r["own"][rows_of(c), at] = out
            return carry

        lax.fori_loop(0, cols // tile, dot_body, 0)
        if not last:
            for way in range(2):

                @pl.when(has_sent(way, 0))
                def _():
                    pass_on(way, 0, c).start()

            put_own(c).start()
        return carry

    lax.fori_loop(0, chunks, chunk_body, 0)
    if last:
        return

    for hop in range(n - 1):

        def forward_body(c, carry):
            for way in range(2):

                @pl.when(has_got(way, hop))
                def _():
                    pass_on(way, hop, c).wait_recv()

                if hop + 1 < n - 1:

                    @pl.when(has_sent(way, hop + 1))
                    def _():
                        pass_on(way, hop + 1, c).start()

            return carry

        lax.fori_loop(0, chunks, forward_body, 0)

    def finish_body(c, carry):
        put_own(c).wait()
        if "stream_out" in r:
            put_stream(c).wait()
        for hop in range(n - 1):
            for way in range(2):

                @pl.when(has_sent(way, hop))
                def _():
                    pass_on(way, hop, c).wait_send()

        return carry

    lax.fori_loop(0, chunks, finish_body, 0)


def run_layer(current, layers, n, stream, branch, gain, weights, counts):
    first, last = current == 0, current + 1 == layers
    rows, width = stream.shape
    cols = weights.shape[1]
    chunks = 2 if last else 4
    part = rows // chunks
    dma = pltpu.SemaphoreType.DMA
    names, args, specs = ["stream"], [stream], [ANY]
    if not first:
        names, args, specs = names + ["branch"], args + [branch], specs + [ANY]
    names, args, specs = (
        names + ["gain", "weights"],
        args + [gain, weights],
        specs + [VMEM, ANY],
    )
    if last:
        names, args, specs = names + ["counts"], args + [counts], specs + [SMEM]
        out_names, out_shape, out_specs = (
            ["mixed"],
            [jax.ShapeDtypeStruct((rows, cols), jnp.bfloat16)],
            [VMEM],
        )
    else:
        out_names, out_shape = ["branch_out"], [jax.ShapeDtypeStruct((rows, width), jnp.bfloat16)]
        if not first:
            out_names = out_names + ["stream_out"]
            out_shape = out_shape + [jax.ShapeDtypeStruct((rows, width), jnp.float32)]
        out_specs = [ANY] * len(out_names)
    scratch = {
        "s": pltpu.VMEM((rows, width), jnp.float32),
        "w": pltpu.VMEM(weights.shape, jnp.bfloat16),
        "x": pltpu.VMEM((part, width), jnp.bfloat16),
        "s_sem": dma((chunks,)),
        "w_sem": dma((4,)),
    }
    if not first:
        scratch["b"] = pltpu.VMEM((rows, width), jnp.bfloat16)
        scratch["b_sem"] = dma((chunks,))
    if not last:
        scratch["own"] = pltpu.VMEM((rows, cols), jnp.bfloat16)
        scratch["own_sem"] = dma((chunks,))
        scratch["send"] = dma((2, n - 1, chunks))
        scratch["recv"] = dma((2, n - 1, chunks))
        if not first:
            scratch["so_sem"] = dma((chunks,))
    size = rows * cols
    out = pl.pallas_call(
        functools.partial(
            layer_kernel, first, last, n, chunks, names + out_names + list(scratch)
        ),
        out_shape=out_shape,
        in_specs=specs,
        out_specs=out_specs,
        scratch_shapes=list(scratch.values()),
        compiler_params=pltpu.CompilerParams(
            collective_id=None if last else 1 + current,
            has_side_effects=not last,
            vmem_limit_bytes=63 * 2**20,
        ),
        cost_estimate=pl.CostEstimate(
            flops=2 * size * width,
            bytes_accessed=(40 if last else 240) * size,
            transcendentals=0,
        ),
        name="last_layer" if last else "layer_%d" % current,
    )(*args)
    if last:
        return None, None, out[0]
    return (stream if first else out[1]), out[0], None


def per_device(
    sizes,
    tokens,
    counts,
    patch_index,
    clip_limit,
    norm_gain,
    params,
    moments,
    seconds,
    gradients,
):
    layers = params.shape[0]
    squares = total_over_mesh(jnp.sum(gradients * gradients), sizes)
    factor = jnp.minimum(1.0, clip_limit / (jnp.sqrt(squares) + 1e-06))
    head = adam_update(params[0], moments[0], seconds[0], gradients[0], factor)[0]
    head = head.astype(jnp.bfloat16)
    later_factor, head, patch_index = lax.optimization_barrier((factor, head, patch_index))
    params_new, moments_new, seconds_new = adam_update(
        params, moments, seconds, gradients, later_factor
    )
    weights = lax.all_gather(head, "dp", axis=0, tiled=True)
    tok_rows = tokens.shape[0]
    valid = lax.broadcasted_iota(jnp.int32, (tok_rows, 1), 0) < counts[0]
    stream = jnp.where(
        valid, tokens.astype(jnp.float32) + position_code(patch_index, tokens.shape[1]), 0.0
    )
    branch = mixed = following = None
    for current in range(layers):
        if current + 1 < layers:
            piece = params_new[current + 1].astype(jnp.bfloat16)
            ready = stream if current == 0 else branch
            piece, weights, ready = lax.optimization_barrier((piece, weights, ready))
            stream, branch = (ready, None) if current == 0 else (stream, ready)
            following = lax.all_gather(piece, "dp", axis=0, tiled=True)
        stream, branch, mixed = run_layer(
            current,
            layers,
            sizes[1],
            stream,
            branch,
            norm_gain[current][None],
            weights,
            counts,
        )
        weights = following
    return (params_new, moments_new, seconds_new, mixed)


def solution(mesh):
    sizes = (mesh.shape["dp"], mesh.shape["fsdp"])
    weight = P(None, "dp", "fsdp")
    return jax.shard_map(
        functools.partial(per_device, sizes),
        mesh=mesh,
        in_specs=(P("dp", None), P("dp"), P("dp"), P(), P(), weight, weight, weight, weight),
        out_specs=(weight, weight, weight, P("dp", "fsdp")),
        check_vma=False,
    )
```

time: 557 us -> 349 us (0.63)
  waiting for transfers between devices: 378 us -> 8.56 us
  Pallas kernels: 0 us -> 264 us
  blocking collectives: 42.2 us -> 0 us
  matrix products: 38.4 us -> 0 us
  other arithmetic: 76.5 us -> 52.6 us
    all_gather x4, waiting for transfers between devices: 378 us -> 8.49 us  [the longest x1 8.43 us: per_device(): weights = lax.all_gather(head, 'dp', axis=0, tiled=True)]
    pallas_call x0 -> x5, Pallas kernels: none -> 264 us  [the longest x4 251 us: run_layer(): pl.pallas_call(functools.partial(layer_kernel, first, last, n, chunks, na...]
    psum x1 -> x0, blocking collectives: 42.2 us -> none  [per_device(): squares = lax.psum(jnp.sum(gradients * gradients), ('dp', 'fsdp'))]
    dot_general x4 -> x0, matrix products: 38.4 us -> none  [per_device(): jnp.dot(normed, gathered[current], preferred_element_type=jnp.float32)]
    reduce_sum x9 -> x1, other arithmetic: 40.9 us -> 6.15 us  [per_device(): squares = total_over_mesh(jnp.sum(gradients * gradients), sizes)]
    another operation x0 -> x1, other arithmetic: none -> 21.4 us
    convert_element_type x1, other arithmetic: 20.8 us -> 6.19 us  [per_device(): head = head.astype(jnp.bfloat16)]
  transfers between devices with their start and end apart: 4 -> 4, of which waited for: 4 -> 1; matrix products, arithmetic and copies ran while one was open for 3% -> 13% of each run, Pallas kernels for 0% -> 67%
where the time goes in v1:
time: 349 us
  Pallas kernels  264 us (76%)
  other arithmetic  52.6 us (15%)
  between operations  15.9 us (5%)
  waiting for transfers between devices  8.56 us (2%)
  local copies, waits for them, and re-layouts  6.94 us (2%)
    pallas_call x4, Pallas kernels, run_layer(): pl.pallas_call(functools.partial(layer_kernel, first, last, n, chunks, na...  251 us
    another operation x1, other arithmetic  21.4 us
    sin x1, other arithmetic, position_code(): jnp.sin(across)  14.7 us
    pallas_call x1, Pallas kernels, total_over_mesh(): pl.pallas_call(functools.partial(total_kernel, sizes), out_shape=jax.Shap...  12.8 us
    all_gather x1, waiting for transfers between devices, per_device(): weights = lax.all_gather(head, 'dp', axis=0, tiled=True)  8.43 us
  transfers between devices with their start and end apart: 4, of which 1 were waited for; matrix products, arithmetic and copies ran while one was open for 13% of the time, Pallas kernels for 67%

profile of v1, /device:TPU:0, one launch (start us, length us, event | category | flops | bytes accessed | tf_op | source)
XLA Modules:
  0.0 348.5 jit_solution(6110501120480873803)
XLA Ops:
  7.2 0.0 all-gather.5.cloned.1.call-start
  7.9 0.0 copy-start.2
  7.9 6.1 %multiply_reduce_fusion = f32[]{:T(128)} fusion(f32[4,512,1024]{2,1,0:T(8,128)} %param.17), kind=kLoop, calls=%fused_computation.6 | loop fusion | flops 4194303 | bytes 8388612 | tf_op jit(solution)/shard_map/reduce_sum | solution.py:367
  14.0 1.2 broadcast_in_dim.19.x_ref
  15.3 12.8 %total.1 = f32[8,128]{1,0:T(8,128)} custom-call(f32[8,128]{1,0:T(8,128)} %broadcast_in_dim.19.x_ref), custom_call_target="tpu_custom_call" | custom-call | tf_op jit(solution)/shard_map/total/pallas_call | solution.py:90
  28.1 1.2 slice.39
  30.0 6.2 %fusion.10 = bf16[512,1024]{1,0:T(8,128)(2,1)} fusion(f32[4,512,1024]{2,1,0:T(8,128)} %param.16, f32[4,512,1024]{2,1,0:T(8,128)} %param.17, f32[4,512,1024]{2,1,0:T(8,128)} %param.15, f32[4,512,1024]{2,1,0:T(8,128)} %param.14, f32[]{:T(128)S(6)} %min.3), kind=kLoop, calls=%fused_computation.23 | loop fusion | flops 8912896 | bytes 9437188 | tf_op jit(solution)/shard_map/convert_element_type | solution.py:370
  36.2 0.0 all-gather.5.cloned.1.call-update
  36.2 0.2 all-gather.7.cloned.1.call-start
  37.1 0.0 copy-done.2
  37.2 21.4 %fusion.14 = (bf16[4,512,1024]{2,1,0:T(8,128)(2,1)}, f32[4,512,1024]{2,1,0:T(8,128)}, f32[4,512,1024]{2,1,0:T(8,128)}, f32[4,512,1024]{2,1,0:T(8,128)}) fusion(f32[4,512,1024]{2,1,0:T(8,128)} %param.14, f32[4,512,1024]{2,1,0:T(8,128)} %param.17, f32[]{:T(128)S(6)} %min.3, f32[4,512,1024]{2,1,0:T(8,128)} %param.15, f32[4,512,1024]{2,1,0:T(8,128)} %param.16), kind=kLoop, calls=%fused_computation.39 | loop fusion | flops 35651584 | bytes 62914564 | tf_op jit(solution)/shard_map/convert.2
  58.6 0.0 copy-start
  58.6 3.8 %slice_bitcast_fusion = (bf16[512,1024]{1,0:T(8,128)(2,1)}, bf16[512,1024]{1,0:T(8,128)(2,1)}, bf16[512,1024]{1,0:T(8,128)(2,1)}) fusion(bf16[4,512,1024]{2,1,0:T(8,128)(2,1)} %get-tuple-element.36), kind=kLoop, calls=%fused_computation.24 | loop fusion | bytes 6291456 | tf_op jit(solution)/shard_map/convert_element_type | solution.py:384
  62.5 14.7 %multiply_sine_fusion.1 = (f32[512,1024]{1,0:T(8,128)S(1)}, f32[512,1024]{1,0:T(8,128)S(1)}, f32[512,1024]{1,0:T(8,128)S(1)}, f32[512,1024]{1,0:T(8,128)S(1)}) fusion(f32[1024]{0:T(1024)S(1)} %negate_power_fusion, f32[512]{0:T(512)S(1)} %get-tuple-element.53, f32[512]{0:T(512)S(1)} %get-tuple-element.54), kind=kLoop, calls=%fused_computation.11 | loop fusion | flops 1048576 | bytes 8396800 | tf_op jit(solution)/shard_map/sin | solution.py:31
  77.2 0.0 copy-done
  77.2 0.0 copy-start.1
  77.2 4.1 %fusion.1.refs_0_ = f32[512,4096]{1,0:T(8,128)} fusion(f32[512,1024]{1,0:T(8,128)S(1)} %get-tuple-element.51, f32[512,1024]{1,0:T(8,128)S(1)} %get-tuple-element.52, f32[512,1024]{1,0:T(8,128)S(1)} %get-tuple-element.48, f32[512,1024]{1,0:T(8,128)S(1)} %get-tuple-element.47, bf16[512,4096]{1,0:T(8,128)(2,1)S(1)} %copy-done, pred[512]{0:T(512)(128)(4,1)S(1)} %iota_compare_fusion), kind=kLoop, calls=%fused_computation.3 | loop fusion | flops 12582912 | bytes 20972032 | tf_op jit(solution)/shard_map/jit(_where)/select_n | solution.py:378
  81.3 8.4 %all-gather.5.cloned.1.call-done.refs_2_ = bf16[4096,1024]{1,0:T(8,128)(2,1)} async-done(((bf16[512,1024]{1,0:T(8,128)(2,1)}), bf16[4096,1024]{1,0:T(8,128)(2,1)}) %all-gather.5.cloned.1.call-update) | async-done | bytes 8388624 | tf_op jit(solution)/shard_map/all_gather | solution.py:375
  89.8 0.0 all-gather.7.cloned.1.call-update
  89.8 0.0 all-gather.9.cloned.1.call-start
  89.8 0.0 copy-done.1
  89.8 0.7 fusion.16
  90.5 78.6 %layer_0.1.refs_1_ = bf16[512,4096]{1,0:T(8,128)(2,1)} custom-call(f32[512,4096]{1,0:T(8,128)} %fusion.1.refs_0_, f32[1,4096]{1,0:T(1,128)} %get-tuple-element.45.refs_1_, bf16[4096,1024]{1,0:T(8,128)(2,1)} %all-gather.5.cloned.1.call-done.refs_2_), custom_call_target="tpu_custom_call" | custom-call | flops 4294967296 | bytes 125829120 | tf_op jit(solution)/shard_map/layer_0/pallas_call | solution.py:329
  169.1 0.0 all-gather.7.cloned.1.call-done.refs_3_
  169.2 0.0 all-gather.9.cloned.1.call-update
  169.2 0.3 all-gather.11.cloned.1.call-start
  169.5 77.9 %layer_1.1 = (bf16[512,4096]{1,0:T(8,128)(2,1)}, f32[512,4096]{1,0:T(8,128)}) custom-call(f32[512,4096]{1,0:T(8,128)} %fusion.1.refs_0_, bf16[512,4096]{1,0:T(8,128)(2,1)} %layer_0.1.refs_1_, f32[1,4096]{1,0:T(1,128)} %get-tuple-element.44.refs_2_, bf16[4096,1024]{1,0:T(8,128)(2,1)} %all-gather.7.cloned.1.call-done.refs_3_), custom_call_target="tpu_custom_call" | custom-call | flops 4294967296 | bytes 125829120 | tf_op jit(solution)/shard_map/layer_1/pallas_call | solution.py:329
  247.4 0.0 all-gather.9.cloned.1.call-done.refs_3_
  247.4 0.0 all-gather.11.cloned.1.call-update
  247.4 77.3 %layer_2.1 = (bf16[512,4096]{1,0:T(8,128)(2,1)}, f32[512,4096]{1,0:T(8,128)}) custom-call(f32[512,4096]{1,0:T(8,128)} %get-tuple-element.28.refs_0_, bf16[512,4096]{1,0:T(8,128)(2,1)} %get-tuple-element.31.refs_1_, f32[1,4096]{1,0:T(1,128)} %get-tuple-element.46.refs_2_, bf16[4096,1024]{1,0:T(8,128)(2,1)} %all-gather.9.cloned.1.call-done.refs_3_), custom_call_target="tpu_custom_call" | custom-call | flops 4294967296 | bytes 125829120 | tf_op jit(solution)/shard_map/layer_2/pallas_call | solution.py:329
  324.7 0.0 all-gather.11.cloned.1.call-done.refs_3_
  324.8 17.2 %last_layer.1 = bf16[512,1024]{1,0:T(8,128)(2,1)} custom-call(f32[512,4096]{1,0:T(8,128)} %get-tuple-element.33.refs_0_, bf16[512,4096]{1,0:T(8,128)(2,1)} %get-tuple-element.34.refs_1_, f32[1,4096]{1,0:T(1,128)} %get-tuple-element.43.refs_2_, bf16[4096,1024]{1,0:T(8,128)(2,1)} %all-gather.11.cloned.1.call-done.refs_3_, s32[1]{0:T(128)} %copy.13.refs_4_), custom_call_target="tpu_custom_call" | custom-call | flops 4294967296 | bytes 20971520 | tf_op jit(solution)/shard_map/last_layer/pallas_call | solution.py:329
  (3 shorter events, 0.0 us)
Async XLA Ops:
  7.2 82.6 %all-gather.5.cloned.1.call-start = ((), (), s32[]{:S(2)}) async-start(), calls=%async_computation | async-start | bytes 9437184 | tf_op jit(solution)/shard_map/all_gather | solution.py:375
  7.9 29.3 %copy-start.2 = (s32[512]{0:T(512)S(1)}, s32[512]{0:T(512)}, u32[]{:S(2)}) copy-start(s32[512]{0:T(512)} %param.11) | copy-start | bytes 6148
  36.2 132.9 %all-gather.7.cloned.1.call-start = ((), (), s32[]{:S(2)}) async-start(), calls=%async_computation.1 | async-start | bytes 9437184 | tf_op jit(solution)/shard_map/all_gather | solution.py:388
  58.6 18.6 %copy-start = (bf16[512,4096]{1,0:T(8,128)(2,1)S(1)}, bf16[512,4096]{1,0:T(8,128)(2,1)}, u32[]{:S(2)}) copy-start(bf16[512,4096]{1,0:T(8,128)(2,1)} %param.9) | copy-start | bytes 12582916
  77.2 12.6 %copy-start.1 = (f32[4,4096]{1,0:T(4,128)S(1)}, f32[4,4096]{1,0:T(4,128)}, u32[]{:S(2)}) copy-start(f32[4,4096]{1,0:T(4,128)} %param.13) | copy-start | bytes 196612
  89.8 157.6 %all-gather.9.cloned.1.call-start = ((), (), s32[]{:S(2)}) async-start(), calls=%async_computation.2 | async-start | bytes 9437184 | tf_op jit(solution)/shard_map/all_gather | solution.py:388
  169.2 155.6 %all-gather.11.cloned.1.call-start = ((), (), s32[]{:S(2)}) async-start(), calls=%async_computation.3 | async-start | bytes 9437184 | tf_op jit(solution)/shard_map/all_gather | solution.py:388
Sparse Core Ops, SparseCore 0:
  36.4 53.3 all-gather.4
  91.6 54.3 all-gather.6
  169.3 53.2 all-gather.8
  247.5 53.2 all-gather.10

commit v2 on v1

--- a/solution.py
+++ b/solution.py
@@ -110,7 +110,10 @@
     rows, width = r["stream"].shape
     cols = r["weights"].shape[1]
     part = rows // chunks
-    depth = r["w"].shape[0] // 4
+    half = cols // 2
+    tile = min(256, half)
+    tiles = cols // tile
+    sub = 32
 
     def rows_of(c):
         return pl.ds(pl.multiple_of(c * part, part), part)
@@ -129,8 +132,10 @@
         )
 
     def take_weights(k):
-        piece = pl.ds(k * depth, depth)
-        return pltpu.make_async_copy(r["weights"].at[piece], r["w"].at[piece], r["w_sem"].at[k])
+        piece = pl.ds(pl.multiple_of(k * tile, tile), tile)
+        return pltpu.make_async_copy(
+            r["weights"].at[:, piece], r["w"].at[:, piece], r["w_sem"].at[k]
+        )
 
     def put_stream(c):
         return pltpu.make_async_copy(
@@ -144,19 +149,18 @@
             r["own_sem"].at[c],
         )
 
-    def pass_on(way, hop, c):
-        if hop == 0:
-            owner = place
-            source = r["own"].at[rows_of(c)]
-        else:
-            owner = place - hop if way == 0 else place + hop
-            source = r["branch_out"].at[rows_of(c), cols_of(owner)]
+    def pass_on(way, hop, c, side):
+        owner = place - hop if way == 0 else place + hop
+        target = r["branch_out"].at[
+            rows_of(c), pl.ds(pl.multiple_of(owner * cols + side * half, half), half)
+        ]
+        source = r["own"].at[rows_of(c), pl.ds(side * half, half)] if hop == 0 else target
         peer = lax.rem(place + 1, n) if way == 0 else lax.rem(place + n - 1, n)
         return pltpu.make_async_remote_copy(
             src_ref=source,
-            dst_ref=r["branch_out"].at[rows_of(c), cols_of(owner)],
-            send_sem=r["send"].at[way, hop, c],
-            recv_sem=r["recv"].at[way, hop, c],
+            dst_ref=target,
+            send_sem=r["send"].at[way, hop, 2 * c + side],
+            recv_sem=r["recv"].at[way, hop, 2 * c + side],
             device_id={"fsdp": peer},
             device_id_type=MESH,
         )
@@ -169,13 +173,14 @@
     def has_got(way, hop):
         return place >= hop + 1 if way == 0 else place + hop + 1 < n
 
-    for c in range(chunks):
+    def take_rows(c):
         take_stream(c).start()
         if not first:
             take_branch(c).start()
-        if c == 0:
-            for k in range(4):
-                take_weights(k).start()
+
+    take_rows(0)
+    for k in range(tiles):
+        take_weights(k).start()
 
     if not last:
         barrier = pltpu.get_barrier_semaphore()
@@ -184,9 +189,6 @@
                 barrier, inc=1, device_id={"fsdp": lax.rem(place + step, n)}, device_id_type=MESH
             )
         pl.semaphore_wait(barrier, 2)
-
-    sub = 32
-    tile = 256
 
     def chunk_body(c, carry):
         take_stream(c).wait()
@@ -210,12 +212,16 @@
         if "stream_out" in r:
             put_stream(c).start()
 
-        @pl.when(c == 0)
-        def _():
-            for k in range(4):
-                take_weights(k).wait()
-
         def dot_body(t, carry):
+            @pl.when(c == 0)
+            def _():
+                take_weights(t).wait()
+
+                @pl.when(t == tiles // 2 - 1)
+                def _():
+                    for later in range(1, chunks):
+                        take_rows(later)
+
             at = pl.ds(pl.multiple_of(t * tile, tile), tile)
             out = jnp.dot(
                 r["x"][...], r["w"][:, at], preferred_element_type=jnp.float32
@@ -230,14 +236,16 @@
                 r["own"][rows_of(c), at] = out
             return carry
 
-        lax.fori_loop(0, cols // tile, dot_body, 0)
+        for side in range(2):
+            lax.fori_loop(side * tiles // 2, (side + 1) * tiles // 2, dot_body, 0)
+            if not last:
+                for way in range(2):
+
+                    @pl.when(has_sent(way, 0))
+                    def _():
+                        pass_on(way, 0, c, side).start()
+
         if not last:
-            for way in range(2):
-
-                @pl.when(has_sent(way, 0))
-                def _():
-                    pass_on(way, 0, c).start()
-
             put_own(c).start()
         return carry
 
@@ -248,17 +256,18 @@
     for hop in range(n - 1):
 
         def forward_body(c, carry):
-            for way in range(2):
-
-                @pl.when(has_got(way, hop))
-                def _():
-                    pass_on(way, hop, c).wait_recv()
-
-                if hop + 1 < n - 1:
-
-                    @pl.when(has_sent(way, hop + 1))
+            for side in range(2):
+                for way in range(2):
+
+                    @pl.when(has_got(way, hop))
                     def _():
-                        pass_on(way, hop + 1, c).start()
+                        pass_on(way, hop, c, side).wait_recv()
+
+                    if hop + 1 < n - 1:
+
+                        @pl.when(has_sent(way, hop + 1))
+                        def _():
+                            pass_on(way, hop + 1, c, side).start()
 
             return carry
 
@@ -273,7 +282,8 @@
 
                 @pl.when(has_sent(way, hop))
                 def _():
-                    pass_on(way, hop, c).wait_send()
+                    for side in range(2):
+                        pass_on(way, hop, c, side).wait_send()
 
         return carry
 
@@ -284,7 +294,7 @@
     first, last = current == 0, current + 1 == layers
     rows, width = stream.shape
     cols = weights.shape[1]
-    chunks = 2 if last else 4
+    chunks = 4
     part = rows // chunks
     dma = pltpu.SemaphoreType.DMA
     names, args, specs = ["stream"], [stream], [ANY]
@@ -313,7 +323,7 @@
         "w": pltpu.VMEM(weights.shape, jnp.bfloat16),
         "x": pltpu.VMEM((part, width), jnp.bfloat16),
         "s_sem": dma((chunks,)),
-        "w_sem": dma((4,)),
+        "w_sem": dma((cols // min(256, cols // 2),)),
     }
     if not first:
         scratch["b"] = pltpu.VMEM((rows, width), jnp.bfloat16)
@@ -321,8 +331,8 @@
     if not last:
         scratch["own"] = pltpu.VMEM((rows, cols), jnp.bfloat16)
         scratch["own_sem"] = dma((chunks,))
-        scratch["send"] = dma((2, n - 1, chunks))
-        scratch["recv"] = dma((2, n - 1, chunks))
+        scratch["send"] = dma((2, n - 1, 2 * chunks))
+        scratch["recv"] = dma((2, n - 1, 2 * chunks))
         if not first:
             scratch["so_sem"] = dma((chunks,))
     size = rows * cols

time: 349 us -> 346 us (level)
  transfers between devices with their start and end apart: 4 -> 4, of which waited for: 1 -> 1; matrix products, arithmetic and copies ran while one was open for 13% -> 13% of each run, Pallas kernels for 67% -> 66%
where the time goes in v2:
time: 346 us
  Pallas kernels  261 us (75%)
  other arithmetic  52.6 us (15%)
  between operations  15.9 us (5%)
  waiting for transfers between devices  8.56 us (2%)
  local copies, waits for them, and re-layouts  6.94 us (2%)
    pallas_call x4, Pallas kernels, run_layer(): pl.pallas_call(functools.partial(layer_kernel, first, last, n, chunks, na...  248 us
    another operation x1, other arithmetic  21.4 us
    sin x1, other arithmetic, position_code(): jnp.sin(across)  14.7 us
    pallas_call x1, Pallas kernels, total_over_mesh(): pl.pallas_call(functools.partial(total_kernel, sizes), out_shape=jax.Shap...  12.8 us
    all_gather x1, waiting for transfers between devices, per_device(): weights = lax.all_gather(head, 'dp', axis=0, tiled=True)  8.43 us
  transfers between devices with their start and end apart: 4, of which 1 were waited for; matrix products, arithmetic and copies ran while one was open for 13% of the time, Pallas kernels for 66%

profile of v2, /device:TPU:0, one launch (start us, length us, event | category | flops | bytes accessed | tf_op | source)
XLA Modules:
  0.0 345.9 jit_solution(1020022632810429146)
XLA Ops:
  7.2 0.0 all-gather.5.cloned.1.call-start
  7.9 0.0 copy-start.2
  7.9 6.1 %multiply_reduce_fusion = f32[]{:T(128)} fusion(f32[4,512,1024]{2,1,0:T(8,128)} %param.17), kind=kLoop, calls=%fused_computation.6 | loop fusion | flops 4194303 | bytes 8388612 | tf_op jit(solution)/shard_map/reduce_sum | solution.py:377
  14.0 1.2 broadcast_in_dim.19.x_ref
  15.3 12.8 %total.1 = f32[8,128]{1,0:T(8,128)} custom-call(f32[8,128]{1,0:T(8,128)} %broadcast_in_dim.19.x_ref), custom_call_target="tpu_custom_call" | custom-call | tf_op jit(solution)/shard_map/total/pallas_call | solution.py:90
  28.1 1.2 slice.39
  30.0 6.2 %fusion.10 = bf16[512,1024]{1,0:T(8,128)(2,1)} fusion(f32[4,512,1024]{2,1,0:T(8,128)} %param.16, f32[4,512,1024]{2,1,0:T(8,128)} %param.17, f32[4,512,1024]{2,1,0:T(8,128)} %param.15, f32[4,512,1024]{2,1,0:T(8,128)} %param.14, f32[]{:T(128)S(6)} %min.3), kind=kLoop, calls=%fused_computation.23 | loop fusion | flops 8912896 | bytes 9437188 | tf_op jit(solution)/shard_map/convert_element_type | solution.py:380
  36.2 0.0 all-gather.5.cloned.1.call-update
  36.2 0.2 all-gather.7.cloned.1.call-start
  37.1 0.0 copy-done.2
  37.2 21.4 %fusion.14 = (bf16[4,512,1024]{2,1,0:T(8,128)(2,1)}, f32[4,512,1024]{2,1,0:T(8,128)}, f32[4,512,1024]{2,1,0:T(8,128)}, f32[4,512,1024]{2,1,0:T(8,128)}) fusion(f32[4,512,1024]{2,1,0:T(8,128)} %param.14, f32[4,512,1024]{2,1,0:T(8,128)} %param.17, f32[]{:T(128)S(6)} %min.3, f32[4,512,1024]{2,1,0:T(8,128)} %param.15, f32[4,512,1024]{2,1,0:T(8,128)} %param.16), kind=kLoop, calls=%fused_computation.39 | loop fusion | flops 35651584 | bytes 62914564 | tf_op jit(solution)/shard_map/convert.2
  58.6 0.0 copy-start
  58.6 3.8 %slice_bitcast_fusion = (bf16[512,1024]{1,0:T(8,128)(2,1)}, bf16[512,1024]{1,0:T(8,128)(2,1)}, bf16[512,1024]{1,0:T(8,128)(2,1)}) fusion(bf16[4,512,1024]{2,1,0:T(8,128)(2,1)} %get-tuple-element.36), kind=kLoop, calls=%fused_computation.24 | loop fusion | bytes 6291456 | tf_op jit(solution)/shard_map/convert_element_type | solution.py:394
  62.5 14.7 %multiply_sine_fusion.1 = (f32[512,1024]{1,0:T(8,128)S(1)}, f32[512,1024]{1,0:T(8,128)S(1)}, f32[512,1024]{1,0:T(8,128)S(1)}, f32[512,1024]{1,0:T(8,128)S(1)}) fusion(f32[1024]{0:T(1024)S(1)} %negate_power_fusion, f32[512]{0:T(512)S(1)} %get-tuple-element.53, f32[512]{0:T(512)S(1)} %get-tuple-element.54), kind=kLoop, calls=%fused_computation.11 | loop fusion | flops 1048576 | bytes 8396800 | tf_op jit(solution)/shard_map/sin | solution.py:31
  77.2 0.0 copy-done
  77.2 0.0 copy-start.1
  77.2 4.1 %fusion.1.refs_0_ = f32[512,4096]{1,0:T(8,128)} fusion(f32[512,1024]{1,0:T(8,128)S(1)} %get-tuple-element.51, f32[512,1024]{1,0:T(8,128)S(1)} %get-tuple-element.52, f32[512,1024]{1,0:T(8,128)S(1)} %get-tuple-element.48, f32[512,1024]{1,0:T(8,128)S(1)} %get-tuple-element.47, bf16[512,4096]{1,0:T(8,128)(2,1)S(1)} %copy-done, pred[512]{0:T(512)(128)(4,1)S(1)} %iota_compare_fusion), kind=kLoop, calls=%fused_computation.3 | loop fusion | flops 12582912 | bytes 20972032 | tf_op jit(solution)/shard_map/jit(_where)/select_n | solution.py:388
  81.3 8.4 %all-gather.5.cloned.1.call-done.refs_2_ = bf16[4096,1024]{1,0:T(8,128)(2,1)} async-done(((bf16[512,1024]{1,0:T(8,128)(2,1)}), bf16[4096,1024]{1,0:T(8,128)(2,1)}) %all-gather.5.cloned.1.call-update) | async-done | bytes 8388624 | tf_op jit(solution)/shard_map/all_gather | solution.py:385
  89.8 0.0 all-gather.7.cloned.1.call-update
  89.8 0.3 all-gather.9.cloned.1.call-start
  90.0 0.0 copy-done.1
  90.1 0.7 fusion.16
  90.7 77.6 %layer_0.1.refs_1_ = bf16[512,4096]{1,0:T(8,128)(2,1)} custom-call(f32[512,4096]{1,0:T(8,128)} %fusion.1.refs_0_, f32[1,4096]{1,0:T(1,128)} %get-tuple-element.45.refs_1_, bf16[4096,1024]{1,0:T(8,128)(2,1)} %all-gather.5.cloned.1.call-done.refs_2_), custom_call_target="tpu_custom_call" | custom-call | flops 4294967296 | bytes 125829120 | tf_op jit(solution)/shard_map/layer_0/pallas_call | solution.py:339
  168.3 0.0 all-gather.7.cloned.1.call-done.refs_3_
  168.3 0.0 all-gather.9.cloned.1.call-update
  168.3 0.0 all-gather.11.cloned.1.call-start
  168.4 75.4 %layer_1.1 = (bf16[512,4096]{1,0:T(8,128)(2,1)}, f32[512,4096]{1,0:T(8,128)}) custom-call(f32[512,4096]{1,0:T(8,128)} %fusion.1.refs_0_, bf16[512,4096]{1,0:T(8,128)(2,1)} %layer_0.1.refs_1_, f32[1,4096]{1,0:T(1,128)} %get-tuple-element.44.refs_2_, bf16[4096,1024]{1,0:T(8,128)(2,1)} %all-gather.7.cloned.1.call-done.refs_3_), custom_call_target="tpu_custom_call" | custom-call | flops 4294967296 | bytes 125829120 | tf_op jit(solution)/shard_map/layer_1/pallas_call | solution.py:339
  243.8 0.0 all-gather.9.cloned.1.call-done.refs_3_
  243.9 0.0 all-gather.11.cloned.1.call-update
  243.9 74.9 %layer_2.1 = (bf16[512,4096]{1,0:T(8,128)(2,1)}, f32[512,4096]{1,0:T(8,128)}) custom-call(f32[512,4096]{1,0:T(8,128)} %get-tuple-element.28.refs_0_, bf16[512,4096]{1,0:T(8,128)(2,1)} %get-tuple-element.31.refs_1_, f32[1,4096]{1,0:T(1,128)} %get-tuple-element.46.refs_2_, bf16[4096,1024]{1,0:T(8,128)(2,1)} %all-gather.9.cloned.1.call-done.refs_3_), custom_call_target="tpu_custom_call" | custom-call | flops 4294967296 | bytes 125829120 | tf_op jit(solution)/shard_map/layer_2/pallas_call | solution.py:339
  318.8 0.0 all-gather.11.cloned.1.call-done.refs_3_
  318.8 20.5 %last_layer.1 = bf16[512,1024]{1,0:T(8,128)(2,1)} custom-call(f32[512,4096]{1,0:T(8,128)} %get-tuple-element.33.refs_0_, bf16[512,4096]{1,0:T(8,128)(2,1)} %get-tuple-element.34.refs_1_, f32[1,4096]{1,0:T(1,128)} %get-tuple-element.43.refs_2_, bf16[4096,1024]{1,0:T(8,128)(2,1)} %all-gather.11.cloned.1.call-done.refs_3_, s32[1]{0:T(128)} %copy.13.refs_4_), custom_call_target="tpu_custom_call" | custom-call | flops 4294967296 | bytes 20971520 | tf_op jit(solution)/shard_map/last_layer/pallas_call | solution.py:339
  (3 shorter events, 0.0 us)
Async XLA Ops:
  7.2 82.6 %all-gather.5.cloned.1.call-start = ((), (), s32[]{:S(2)}) async-start(), calls=%async_computation | async-start | bytes 9437184 | tf_op jit(solution)/shard_map/all_gather | solution.py:385
  7.9 29.3 %copy-start.2 = (s32[512]{0:T(512)S(1)}, s32[512]{0:T(512)}, u32[]{:S(2)}) copy-start(s32[512]{0:T(512)} %param.11) | copy-start | bytes 6148
  36.2 132.1 %all-gather.7.cloned.1.call-start = ((), (), s32[]{:S(2)}) async-start(), calls=%async_computation.1 | async-start | bytes 9437184 | tf_op jit(solution)/shard_map/all_gather | solution.py:398
  58.6 18.6 %copy-start = (bf16[512,4096]{1,0:T(8,128)(2,1)S(1)}, bf16[512,4096]{1,0:T(8,128)(2,1)}, u32[]{:S(2)}) copy-start(bf16[512,4096]{1,0:T(8,128)(2,1)} %param.9) | copy-start | bytes 12582916
  77.2 12.9 %copy-start.1 = (f32[4,4096]{1,0:T(4,128)S(1)}, f32[4,4096]{1,0:T(4,128)}, u32[]{:S(2)}) copy-start(f32[4,4096]{1,0:T(4,128)} %param.13) | copy-start | bytes 196612
  89.8 154.1 %all-gather.9.cloned.1.call-start = ((), (), s32[]{:S(2)}) async-start(), calls=%async_computation.2 | async-start | bytes 9437184 | tf_op jit(solution)/shard_map/all_gather | solution.py:398
  168.3 150.4 %all-gather.11.cloned.1.call-start = ((), (), s32[]{:S(2)}) async-start(), calls=%async_computation.3 | async-start | bytes 9437184 | tf_op jit(solution)/shard_map/all_gather | solution.py:398
Sparse Core Ops, SparseCore 0:
  36.4 53.3 all-gather.4
  91.6 54.2 all-gather.6
  168.4 53.3 all-gather.8
  244.0 53.2 all-gather.10
